TPU v7x, 256 devices: a whole 4x4x8 slice. The times are simulated.
256 devices in a mesh: section: 16 (over x, y), tensor: 16 (over z, core).
Axes of the slice: x: 4, y: 4, z: 8, core: 2. Of those that a mesh axis runs over, the one named last changes fastest.
Arguments:
- token_ids: int32 [3, 48], replicated, may hold values from 0 to 31999
- emb_table: bfloat16 [32000, 4096], P('section', 'tensor'), may hold values from -6 to 6
- attn_gain: bfloat16 [16, 4096], P('section'), may hold values from 0.25 to 1.75
- query_weight: bfloat16 [16, 4096, 4096], P('section', None, 'tensor'), may hold values from -8 to 8
- key_weight: bfloat16 [16, 4096, 4096], P('section', None, 'tensor'), may hold values from -8 to 8
- value_weight: bfloat16 [16, 4096, 4096], P('section', None, 'tensor'), may hold values from -0.09375 to 0.09375
- mix_weight: float32 [16, 32], P('section', 'tensor'), may hold values from 0.2 to 0.8
- out_weight: bfloat16 [16, 4096, 4096], P('section', 'tensor'), may hold values from -0.125 to 0.125
Outputs:
- layer_outputs: bfloat16 [16, 3, 48, 4096], P('section', None, None, 'tensor')
All inputs are finite; a program needn't handle non-finite values.
Results may differ from a plain program's by a relative error of at most 0.033.
Values may be sent and summed in bfloat16 or wider, within the bound.
No kernel may reach another device: no remote copies, remote signals or barrier semaphores. Data moves between devices by JAX's collectives and lax.ppermute only.
A program may use at most 64 MiB of HBM per device.

v0:
```python
import jax
import jax.numpy as jnp
from jax import lax
from jax.sharding import PartitionSpec as P

EPSILON = 1e-05
ROTARY_BASE = 10000.0


def from_everyone(array, axis):
    peers = lax.axis_size(axis)
    return lax.all_to_all(
        jnp.broadcast_to(array[None], (peers, *array.shape)), axis, 0, 0, tiled=True
    )


def of_everyone(array, axis):
    return from_everyone(array, axis).astype(jnp.float32).sum(axis=0)


def broadcast(array, axis, root):
    return lax.dynamic_index_in_dim(lax.all_gather(array, axis), root, 0, keepdims=False)


def laid_out(pieces, dim):
    lengths = list(pieces.shape[1:])
    lengths[dim] *= pieces.shape[0]
    return jnp.moveaxis(pieces, 0, dim).reshape(lengths)


def gather_directly(array, axis, dim):
    return laid_out(from_everyone(array, axis), dim)


def in_blocks(array, dim, peers):
    lengths = array.shape
    pieces = array.reshape(*lengths[:dim], peers, lengths[dim] // peers, *lengths[dim + 1 :])
    return jnp.moveaxis(pieces, dim, 0)


def summed_on_arrival(array, axis, dim):
    pieces = in_blocks(array, dim, lax.axis_size(axis))
    arrived = lax.all_to_all(pieces, axis, split_axis=0, concat_axis=0, tiled=True)
    return arrived.astype(jnp.float32).sum(axis=0)


def shifted(value, axis, steps):
    count = lax.axis_size(axis)
    first, last = (max(0, -steps), min(count, count - steps))
    return lax.ppermute(value, axis, [(source, source + steps) for source in range(first, last)])


def rms_scale(values, norm_gain):
    mean_square = jnp.mean(values * values, axis=-1, keepdims=True)
    return values * lax.rsqrt(mean_square + EPSILON) * norm_gain


def rotate(values):
    length = values.shape[-3]
    head_dim = values.shape[-1]
    half_dim = head_dim // 2
    positions = jnp.arange(length, dtype=jnp.float32)
    frequency = ROTARY_BASE ** (-(jnp.arange(half_dim, dtype=jnp.float32) * 2.0) / head_dim)
    angles = positions[:, None] * frequency[None, :]
    cosine = jnp.cos(angles)[:, None, :]
    sine_table = jnp.sin(angles)[:, None, :]
    leading = values[..., :half_dim]
    second = values[..., half_dim:]
    return jnp.concatenate(
        [leading * cosine - second * sine_table, second * cosine + leading * sine_table], axis=-1
    )


def attend(queries, key_rows, mixed_values):
    length = queries.shape[0]
    head_dim = queries.shape[2]
    scores = jnp.einsum(
        "qhd,khd->hqk", queries, key_rows, preferred_element_type=jnp.float32
    ) * head_dim ** (-0.5)
    causal = jnp.arange(length)[:, None] >= jnp.arange(length)[None, :]
    scores = jnp.where(causal, scores, -1e30)
    row_top = jnp.max(scores, axis=-1, keepdims=True)
    expo = jnp.exp(scores - row_top)
    attn_probs = (expo / jnp.sum(expo, axis=-1, keepdims=True)).astype(jnp.bfloat16)
    attended = jnp.einsum(
        "hqk,khd->qhd", attn_probs, mixed_values, preferred_element_type=jnp.float32
    )
    return attended.astype(jnp.bfloat16)


def shards(
    token_ids, emb_table, attn_gain, query_weight, key_weight, value_weight, mix_weight, out_weight
):
    section_rank = lax.axis_index("section")
    section_count = lax.axis_size("section")
    batches, length = token_ids.shape
    vocab_local, width_local = emb_table.shape
    head_local = mix_weight.shape[1]
    head_dim = query_weight.shape[2] // head_local
    norm_gain = attn_gain[0].astype(jnp.float32)
    w_query = query_weight[0]
    w_key = key_weight[0]
    w_value = value_weight[0]
    w_out = out_weight[0]
    mix_rate = mix_weight[0][None, :, None]
    flat_ids = token_ids.reshape(-1) - section_rank * vocab_local
    one_hot = (flat_ids[:, None] == jnp.arange(vocab_local, dtype=jnp.int32)[None, :]).astype(
        jnp.bfloat16
    )
    looked = jnp.dot(one_hot, emb_table, preferred_element_type=jnp.float32)
    first_shard = (
        of_everyone(looked.astype(jnp.bfloat16), "section").astype(jnp.float32).astype(jnp.bfloat16)
    )
    first_full = lax.all_gather(first_shard, "tensor", axis=1, tiled=True)
    first_float = first_full.astype(jnp.float32)

    def root_project():
        first_norm = rms_scale(first_float, norm_gain).astype(jnp.bfloat16)
        return jnp.dot(first_norm, w_value, preferred_element_type=jnp.float32).astype(jnp.bfloat16)

    def skipped():
        return jnp.zeros((first_full.shape[0], w_value.shape[1]), jnp.bfloat16)

    own_values = lax.cond(section_rank == 0, root_project, skipped)
    first_values = broadcast(own_values, "section", 0)
    source_values = first_values.reshape(batches, length, head_local, head_dim)
    first_blocks = first_shard.reshape(batches, length, width_local)

    def attention_branch(full_rows, micro_index):
        normed = rms_scale(full_rows.astype(jnp.float32), norm_gain).astype(jnp.bfloat16)
        queries = jnp.dot(normed, w_query, preferred_element_type=jnp.float32)
        key_rows = jnp.dot(normed, w_key, preferred_element_type=jnp.float32)
        values = jnp.dot(normed, w_value, preferred_element_type=jnp.float32)
        queries = rotate(queries.reshape(length, head_local, head_dim)).astype(jnp.bfloat16)
        key_rows = rotate(key_rows.reshape(length, head_local, head_dim)).astype(jnp.bfloat16)
        values = values.reshape(length, head_local, head_dim)
        picked = lax.dynamic_index_in_dim(source_values, micro_index, 0, keepdims=False).astype(
            jnp.float32
        )
        mixed_values = (mix_rate * values + (1.0 - mix_rate) * picked).astype(jnp.bfloat16)
        attended = attend(queries, key_rows, mixed_values).reshape(length, head_local * head_dim)
        return jnp.dot(attended, w_out, preferred_element_type=jnp.float32)

    def advance(step_index, loop_state):
        incoming, outputs = loop_state
        position = step_index - section_rank
        is_valid = (position >= 0) & (position < batches)
        micro_index = jnp.clip(position, 0, batches - 1)
        starting = lax.dynamic_index_in_dim(first_blocks, micro_index, 0, keepdims=False)
        shard_rows = jnp.where(section_rank == 0, starting, incoming)
        full_rows = gather_directly(shard_rows, "tensor", 1)
        summed = summed_on_arrival(
            attention_branch(full_rows, micro_index).astype(jnp.bfloat16), "tensor", 1
        )
        fresh_rows = (shard_rows.astype(jnp.float32) + summed).astype(jnp.bfloat16)
        previous = lax.dynamic_index_in_dim(outputs, micro_index, 0, keepdims=False)
        kept_rows = jnp.where(is_valid, fresh_rows, previous)
        outputs = lax.dynamic_update_index_in_dim(outputs, kept_rows, micro_index, 0)
        incoming = shifted(fresh_rows, "section", 1)
        return (incoming, outputs)

    incoming = jnp.zeros((length, width_local), jnp.bfloat16)
    outputs = jnp.zeros((batches, length, width_local), jnp.bfloat16)
    step_count = batches + section_count - 1
    incoming, outputs = lax.fori_loop(0, step_count, advance, (incoming, outputs))
    return outputs[None]


def solution(mesh):
    in_specs = (
        P(),
        P("section", "tensor"),
        P("section", None),
        P("section", None, "tensor"),
        P("section", None, "tensor"),
        P("section", None, "tensor"),
        P("section", "tensor"),
        P("section", "tensor", None),
    )
    out_specs = P("section", None, None, "tensor")
    return jax.shard_map(shards, mesh=mesh, in_specs=in_specs, out_specs=out_specs, check_vma=False)
```

profile of v0, /device:TPU:3, one launch (start us, length us, event | category | flops | bytes accessed | tf_op | source)
XLA Modules:
  0.0 1204.4 jit_solution(4408953827602636049)
XLA Ops:
  8.2 23.0 %all_to_all.29 = bf16[16,144,256]{2,1,0:T(8,128)(2,1)} all-to-all(bf16[16,144,256]{2,1,0:T(8,128)(2,1)S(1)} %broadcast_in_dim.99), channel_id=1, replica_groups=mesh['section'=16,'tensor'=16] {'section'}, dimensions={0} | all-to-all | bytes 2359296 | tf_op jit(solution)/shard_map/all_to_all | solution.py:12
  36.4 37.1 %all-gather.4.cloned.1.call-done = bf16[144,4096]{1,0:T(8,128)(2,1)} async-done(((bf16[144,256]{1,0:T(8,128)(2,1)}), bf16[144,4096]{1,0:T(8,128)(2,1)}) %all-gather.4.cloned.1.call-update) | async-done | bytes 1179664 | tf_op jit(solution)/shard_map/all_gather | solution.py:114
  85.4 36.8 %all-gather.6.cloned.1.call-done = bf16[2304,256]{1,0:T(8,128)(2,1)} async-done(((bf16[144,256]{1,0:T(8,128)(2,1)}), bf16[2304,256]{1,0:T(8,128)(2,1)}) %all-gather.6.cloned.1.call-update) | async-done | bytes 1179664 | tf_op jit(solution)/shard_map/all_gather | solution.py:22
  124.4 1073.2 %while.17 = (s32[]{:T(128)}, bf16[48,256]{1,0:T(8,128)(2,1)S(1)}, bf16[3,48,256]{2,1,0:T(8,128)(2,1)}, pred[]{:T(512)}, s32[]{:T(128)}, /*index=5*/bf16[3,48,256...) while((s32[]{:T(128)}, bf16[48,256]{1,0:T(8,128)(2,1)S(1)}, ...), condition=%wide.wide.region_9.10_spmd, body=%wide.wide.region_4.9_spmd.sunk | while | flops 407331392 | bytes 26102732 | solution.py:165
  168.0 12.5 %all-to-all-done.1 = bf16[16,48,256]{2,1,0:T(8,128)(2,1)S(1)} async-done(((bf16[16,48,256]{2,1,0:T(8,128)(2,1)}), bf16[16,48,256]{2,1,0:T(8,128)(2,1)S(1)}, u32[]{:S(2)}, u32[]{:S(2)}) %all-to-all-start.1) | async-done | bytes 393248 | tf_op jit(solution)/shard_map/while/body/eval_jaxpr/all_to_all | solution.py:43
  198.2 10.5 all-to-all-done
  227.4 12.5 %all-to-all-done.1 = bf16[16,48,256]{2,1,0:T(8,128)(2,1)S(1)} async-done(((bf16[16,48,256]{2,1,0:T(8,128)(2,1)}), bf16[16,48,256]{2,1,0:T(8,128)(2,1)S(1)}, u32[]{:S(2)}, u32[]{:S(2)}) %all-to-all-start.1) | async-done | bytes 393248 | tf_op jit(solution)/shard_map/while/body/eval_jaxpr/all_to_all | solution.py:43
  286.7 12.5 %all-to-all-done.1 = bf16[16,48,256]{2,1,0:T(8,128)(2,1)S(1)} async-done(((bf16[16,48,256]{2,1,0:T(8,128)(2,1)}), bf16[16,48,256]{2,1,0:T(8,128)(2,1)S(1)}, u32[]{:S(2)}, u32[]{:S(2)}) %all-to-all-start.1) | async-done | bytes 393248 | tf_op jit(solution)/shard_map/while/body/eval_jaxpr/all_to_all | solution.py:43
  316.9 10.5 all-to-all-done
  346.0 12.5 %all-to-all-done.1 = bf16[16,48,256]{2,1,0:T(8,128)(2,1)S(1)} async-done(((bf16[16,48,256]{2,1,0:T(8,128)(2,1)}), bf16[16,48,256]{2,1,0:T(8,128)(2,1)S(1)}, u32[]{:S(2)}, u32[]{:S(2)}) %all-to-all-start.1) | async-done | bytes 393248 | tf_op jit(solution)/shard_map/while/body/eval_jaxpr/all_to_all | solution.py:43
  405.4 12.5 %all-to-all-done.1 = bf16[16,48,256]{2,1,0:T(8,128)(2,1)S(1)} async-done(((bf16[16,48,256]{2,1,0:T(8,128)(2,1)}), bf16[16,48,256]{2,1,0:T(8,128)(2,1)S(1)}, u32[]{:S(2)}, u32[]{:S(2)}) %all-to-all-start.1) | async-done | bytes 393248 | tf_op jit(solution)/shard_map/while/body/eval_jaxpr/all_to_all | solution.py:43
  464.7 12.5 %all-to-all-done.1 = bf16[16,48,256]{2,1,0:T(8,128)(2,1)S(1)} async-done(((bf16[16,48,256]{2,1,0:T(8,128)(2,1)}), bf16[16,48,256]{2,1,0:T(8,128)(2,1)S(1)}, u32[]{:S(2)}, u32[]{:S(2)}) %all-to-all-start.1) | async-done | bytes 393248 | tf_op jit(solution)/shard_map/while/body/eval_jaxpr/all_to_all | solution.py:43
  524.0 12.5 %all-to-all-done.1 = bf16[16,48,256]{2,1,0:T(8,128)(2,1)S(1)} async-done(((bf16[16,48,256]{2,1,0:T(8,128)(2,1)}), bf16[16,48,256]{2,1,0:T(8,128)(2,1)S(1)}, u32[]{:S(2)}, u32[]{:S(2)}) %all-to-all-start.1) | async-done | bytes 393248 | tf_op jit(solution)/shard_map/while/body/eval_jaxpr/all_to_all | solution.py:43
  583.4 12.5 %all-to-all-done.1 = bf16[16,48,256]{2,1,0:T(8,128)(2,1)S(1)} async-done(((bf16[16,48,256]{2,1,0:T(8,128)(2,1)}), bf16[16,48,256]{2,1,0:T(8,128)(2,1)S(1)}, u32[]{:S(2)}, u32[]{:S(2)}) %all-to-all-start.1) | async-done | bytes 393248 | tf_op jit(solution)/shard_map/while/body/eval_jaxpr/all_to_all | solution.py:43
  642.7 12.5 %all-to-all-done.1 = bf16[16,48,256]{2,1,0:T(8,128)(2,1)S(1)} async-done(((bf16[16,48,256]{2,1,0:T(8,128)(2,1)}), bf16[16,48,256]{2,1,0:T(8,128)(2,1)S(1)}, u32[]{:S(2)}, u32[]{:S(2)}) %all-to-all-start.1) | async-done | bytes 393248 | tf_op jit(solution)/shard_map/while/body/eval_jaxpr/all_to_all | solution.py:43
  702.0 12.5 %all-to-all-done.1 = bf16[16,48,256]{2,1,0:T(8,128)(2,1)S(1)} async-done(((bf16[16,48,256]{2,1,0:T(8,128)(2,1)}), bf16[16,48,256]{2,1,0:T(8,128)(2,1)S(1)}, u32[]{:S(2)}, u32[]{:S(2)}) %all-to-all-start.1) | async-done | bytes 393248 | tf_op jit(solution)/shard_map/while/body/eval_jaxpr/all_to_all | solution.py:43
  761.4 12.5 %all-to-all-done.1 = bf16[16,48,256]{2,1,0:T(8,128)(2,1)S(1)} async-done(((bf16[16,48,256]{2,1,0:T(8,128)(2,1)}), bf16[16,48,256]{2,1,0:T(8,128)(2,1)S(1)}, u32[]{:S(2)}, u32[]{:S(2)}) %all-to-all-start.1) | async-done | bytes 393248 | tf_op jit(solution)/shard_map/while/body/eval_jaxpr/all_to_all | solution.py:43
  820.7 12.5 %all-to-all-done.1 = bf16[16,48,256]{2,1,0:T(8,128)(2,1)S(1)} async-done(((bf16[16,48,256]{2,1,0:T(8,128)(2,1)}), bf16[16,48,256]{2,1,0:T(8,128)(2,1)S(1)}, u32[]{:S(2)}, u32[]{:S(2)}) %all-to-all-start.1) | async-done | bytes 393248 | tf_op jit(solution)/shard_map/while/body/eval_jaxpr/all_to_all | solution.py:43
  880.0 12.5 %all-to-all-done.1 = bf16[16,48,256]{2,1,0:T(8,128)(2,1)S(1)} async-done(((bf16[16,48,256]{2,1,0:T(8,128)(2,1)}), bf16[16,48,256]{2,1,0:T(8,128)(2,1)S(1)}, u32[]{:S(2)}, u32[]{:S(2)}) %all-to-all-start.1) | async-done | bytes 393248 | tf_op jit(solution)/shard_map/while/body/eval_jaxpr/all_to_all | solution.py:43
  939.4 12.5 %all-to-all-done.1 = bf16[16,48,256]{2,1,0:T(8,128)(2,1)S(1)} async-done(((bf16[16,48,256]{2,1,0:T(8,128)(2,1)}), bf16[16,48,256]{2,1,0:T(8,128)(2,1)S(1)}, u32[]{:S(2)}, u32[]{:S(2)}) %all-to-all-start.1) | async-done | bytes 393248 | tf_op jit(solution)/shard_map/while/body/eval_jaxpr/all_to_all | solution.py:43
  998.7 12.5 %all-to-all-done.1 = bf16[16,48,256]{2,1,0:T(8,128)(2,1)S(1)} async-done(((bf16[16,48,256]{2,1,0:T(8,128)(2,1)}), bf16[16,48,256]{2,1,0:T(8,128)(2,1)S(1)}, u32[]{:S(2)}, u32[]{:S(2)}) %all-to-all-start.1) | async-done | bytes 393248 | tf_op jit(solution)/shard_map/while/body/eval_jaxpr/all_to_all | solution.py:43
  1058.1 12.5 %all-to-all-done.1 = bf16[16,48,256]{2,1,0:T(8,128)(2,1)S(1)} async-done(((bf16[16,48,256]{2,1,0:T(8,128)(2,1)}), bf16[16,48,256]{2,1,0:T(8,128)(2,1)S(1)}, u32[]{:S(2)}, u32[]{:S(2)}) %all-to-all-start.1) | async-done | bytes 393248 | tf_op jit(solution)/shard_map/while/body/eval_jaxpr/all_to_all | solution.py:43
  1117.4 12.5 %all-to-all-done.1 = bf16[16,48,256]{2,1,0:T(8,128)(2,1)S(1)} async-done(((bf16[16,48,256]{2,1,0:T(8,128)(2,1)}), bf16[16,48,256]{2,1,0:T(8,128)(2,1)S(1)}, u32[]{:S(2)}, u32[]{:S(2)}) %all-to-all-start.1) | async-done | bytes 393248 | tf_op jit(solution)/shard_map/while/body/eval_jaxpr/all_to_all | solution.py:43
  1176.7 12.5 %all-to-all-done.1 = bf16[16,48,256]{2,1,0:T(8,128)(2,1)S(1)} async-done(((bf16[16,48,256]{2,1,0:T(8,128)(2,1)}), bf16[16,48,256]{2,1,0:T(8,128)(2,1)S(1)}, u32[]{:S(2)}, u32[]{:S(2)}) %all-to-all-start.1) | async-done | bytes 393248 | tf_op jit(solution)/shard_map/while/body/eval_jaxpr/all_to_all | solution.py:43
  (621 shorter events, 845.0 us)
Async XLA Ops:
  6.5 67.0 %all-gather.4.cloned.1.call-start = ((), (), s32[]{:S(2)}) async-start(), calls=%async_computation.3 | async-start | bytes 1253376 | tf_op jit(solution)/shard_map/all_gather | solution.py:114
  33.4 88.8 %all-gather.6.cloned.1.call-start = ((), (), s32[]{:S(2)}) async-start(), calls=%async_computation.4 | async-start | bytes 1253376 | tf_op jit(solution)/shard_map/all_gather | solution.py:22
  125.9 23.5 %all-to-all-start = ((bf16[16,48,256]{2,1,0:T(8,128)(2,1)}), bf16[16,48,256]{2,1,0:T(8,128)(2,1)S(1)}, u32[]{:S(2)}, u32[]{:S(2)}) async-start(bf16[16,48,256]{2,1,0:T(8,128)(2,1)} %broadcast_in_dim.123), calls=%async_computation | async-start | bytes 786432 | tf_op jit(solution)/shard_map/while/body/eval_jaxpr/all_to_all | solution.py:12
  190.4 18.3 %all-to-all-start = ((bf16[16,48,256]{2,1,0:T(8,128)(2,1)}), bf16[16,48,256]{2,1,0:T(8,128)(2,1)S(1)}, u32[]{:S(2)}, u32[]{:S(2)}) async-start(bf16[16,48,256]{2,1,0:T(8,128)(2,1)} %broadcast_in_dim.123), calls=%async_computation | async-start | bytes 786432 | tf_op jit(solution)/shard_map/while/body/eval_jaxpr/all_to_all | solution.py:12
  249.7 18.3 %all-to-all-start = ((bf16[16,48,256]{2,1,0:T(8,128)(2,1)}), bf16[16,48,256]{2,1,0:T(8,128)(2,1)S(1)}, u32[]{:S(2)}, u32[]{:S(2)}) async-start(bf16[16,48,256]{2,1,0:T(8,128)(2,1)} %broadcast_in_dim.123), calls=%async_computation | async-start | bytes 786432 | tf_op jit(solution)/shard_map/while/body/eval_jaxpr/all_to_all | solution.py:12
  309.1 18.3 %all-to-all-start = ((bf16[16,48,256]{2,1,0:T(8,128)(2,1)}), bf16[16,48,256]{2,1,0:T(8,128)(2,1)S(1)}, u32[]{:S(2)}, u32[]{:S(2)}) async-start(bf16[16,48,256]{2,1,0:T(8,128)(2,1)} %broadcast_in_dim.123), calls=%async_computation | async-start | bytes 786432 | tf_op jit(solution)/shard_map/while/body/eval_jaxpr/all_to_all | solution.py:12
  368.4 18.3 %all-to-all-start = ((bf16[16,48,256]{2,1,0:T(8,128)(2,1)}), bf16[16,48,256]{2,1,0:T(8,128)(2,1)S(1)}, u32[]{:S(2)}, u32[]{:S(2)}) async-start(bf16[16,48,256]{2,1,0:T(8,128)(2,1)} %broadcast_in_dim.123), calls=%async_computation | async-start | bytes 786432 | tf_op jit(solution)/shard_map/while/body/eval_jaxpr/all_to_all | solution.py:12
  400.5 17.4 %all-to-all-start.1 = ((bf16[16,48,256]{2,1,0:T(8,128)(2,1)}), bf16[16,48,256]{2,1,0:T(8,128)(2,1)S(1)}, u32[]{:S(2)}, u32[]{:S(2)}) async-start(bf16[16,48,256]{2,1,0:T(8,128)(2,1)} %bitcast.132), calls=%async_computation.1 | async-start | bytes 786432 | tf_op jit(solution)/shard_map/while/body/eval_jaxpr/all_to_all | solution.py:43
  427.8 18.3 %all-to-all-start = ((bf16[16,48,256]{2,1,0:T(8,128)(2,1)}), bf16[16,48,256]{2,1,0:T(8,128)(2,1)S(1)}, u32[]{:S(2)}, u32[]{:S(2)}) async-start(bf16[16,48,256]{2,1,0:T(8,128)(2,1)} %broadcast_in_dim.123), calls=%async_computation | async-start | bytes 786432 | tf_op jit(solution)/shard_map/while/body/eval_jaxpr/all_to_all | solution.py:12
  487.1 18.3 %all-to-all-start = ((bf16[16,48,256]{2,1,0:T(8,128)(2,1)}), bf16[16,48,256]{2,1,0:T(8,128)(2,1)S(1)}, u32[]{:S(2)}, u32[]{:S(2)}) async-start(bf16[16,48,256]{2,1,0:T(8,128)(2,1)} %broadcast_in_dim.123), calls=%async_computation | async-start | bytes 786432 | tf_op jit(solution)/shard_map/while/body/eval_jaxpr/all_to_all | solution.py:12
  519.2 17.4 %all-to-all-start.1 = ((bf16[16,48,256]{2,1,0:T(8,128)(2,1)}), bf16[16,48,256]{2,1,0:T(8,128)(2,1)S(1)}, u32[]{:S(2)}, u32[]{:S(2)}) async-start(bf16[16,48,256]{2,1,0:T(8,128)(2,1)} %bitcast.132), calls=%async_computation.1 | async-start | bytes 786432 | tf_op jit(solution)/shard_map/while/body/eval_jaxpr/all_to_all | solution.py:43
  546.4 18.3 %all-to-all-start = ((bf16[16,48,256]{2,1,0:T(8,128)(2,1)}), bf16[16,48,256]{2,1,0:T(8,128)(2,1)S(1)}, u32[]{:S(2)}, u32[]{:S(2)}) async-start(bf16[16,48,256]{2,1,0:T(8,128)(2,1)} %broadcast_in_dim.123), calls=%async_computation | async-start | bytes 786432 | tf_op jit(solution)/shard_map/while/body/eval_jaxpr/all_to_all | solution.py:12
  605.7 18.3 %all-to-all-start = ((bf16[16,48,256]{2,1,0:T(8,128)(2,1)}), bf16[16,48,256]{2,1,0:T(8,128)(2,1)S(1)}, u32[]{:S(2)}, u32[]{:S(2)}) async-start(bf16[16,48,256]{2,1,0:T(8,128)(2,1)} %broadcast_in_dim.123), calls=%async_computation | async-start | bytes 786432 | tf_op jit(solution)/shard_map/while/body/eval_jaxpr/all_to_all | solution.py:12
  665.1 18.3 %all-to-all-start = ((bf16[16,48,256]{2,1,0:T(8,128)(2,1)}), bf16[16,48,256]{2,1,0:T(8,128)(2,1)S(1)}, u32[]{:S(2)}, u32[]{:S(2)}) async-start(bf16[16,48,256]{2,1,0:T(8,128)(2,1)} %broadcast_in_dim.123), calls=%async_computation | async-start | bytes 786432 | tf_op jit(solution)/shard_map/while/body/eval_jaxpr/all_to_all | solution.py:12
  724.4 18.3 %all-to-all-start = ((bf16[16,48,256]{2,1,0:T(8,128)(2,1)}), bf16[16,48,256]{2,1,0:T(8,128)(2,1)S(1)}, u32[]{:S(2)}, u32[]{:S(2)}) async-start(bf16[16,48,256]{2,1,0:T(8,128)(2,1)} %broadcast_in_dim.123), calls=%async_computation | async-start | bytes 786432 | tf_op jit(solution)/shard_map/while/body/eval_jaxpr/all_to_all | solution.py:12
  756.6 17.4 %all-to-all-start.1 = ((bf16[16,48,256]{2,1,0:T(8,128)(2,1)}), bf16[16,48,256]{2,1,0:T(8,128)(2,1)S(1)}, u32[]{:S(2)}, u32[]{:S(2)}) async-start(bf16[16,48,256]{2,1,0:T(8,128)(2,1)} %bitcast.132), calls=%async_computation.1 | async-start | bytes 786432 | tf_op jit(solution)/shard_map/while/body/eval_jaxpr/all_to_all | solution.py:43
  783.8 18.3 %all-to-all-start = ((bf16[16,48,256]{2,1,0:T(8,128)(2,1)}), bf16[16,48,256]{2,1,0:T(8,128)(2,1)S(1)}, u32[]{:S(2)}, u32[]{:S(2)}) async-start(bf16[16,48,256]{2,1,0:T(8,128)(2,1)} %broadcast_in_dim.123), calls=%async_computation | async-start | bytes 786432 | tf_op jit(solution)/shard_map/while/body/eval_jaxpr/all_to_all | solution.py:12
  843.1 18.3 %all-to-all-start = ((bf16[16,48,256]{2,1,0:T(8,128)(2,1)}), bf16[16,48,256]{2,1,0:T(8,128)(2,1)S(1)}, u32[]{:S(2)}, u32[]{:S(2)}) async-start(bf16[16,48,256]{2,1,0:T(8,128)(2,1)} %broadcast_in_dim.123), calls=%async_computation | async-start | bytes 786432 | tf_op jit(solution)/shard_map/while/body/eval_jaxpr/all_to_all | solution.py:12
  875.2 17.4 %all-to-all-start.1 = ((bf16[16,48,256]{2,1,0:T(8,128)(2,1)}), bf16[16,48,256]{2,1,0:T(8,128)(2,1)S(1)}, u32[]{:S(2)}, u32[]{:S(2)}) async-start(bf16[16,48,256]{2,1,0:T(8,128)(2,1)} %bitcast.132), calls=%async_computation.1 | async-start | bytes 786432 | tf_op jit(solution)/shard_map/while/body/eval_jaxpr/all_to_all | solution.py:43
  902.4 18.3 %all-to-all-start = ((bf16[16,48,256]{2,1,0:T(8,128)(2,1)}), bf16[16,48,256]{2,1,0:T(8,128)(2,1)S(1)}, u32[]{:S(2)}, u32[]{:S(2)}) async-start(bf16[16,48,256]{2,1,0:T(8,128)(2,1)} %broadcast_in_dim.123), calls=%async_computation | async-start | bytes 786432 | tf_op jit(solution)/shard_map/while/body/eval_jaxpr/all_to_all | solution.py:12
  961.7 18.3 %all-to-all-start = ((bf16[16,48,256]{2,1,0:T(8,128)(2,1)}), bf16[16,48,256]{2,1,0:T(8,128)(2,1)S(1)}, u32[]{:S(2)}, u32[]{:S(2)}) async-start(bf16[16,48,256]{2,1,0:T(8,128)(2,1)} %broadcast_in_dim.123), calls=%async_computation | async-start | bytes 786432 | tf_op jit(solution)/shard_map/while/body/eval_jaxpr/all_to_all | solution.py:12
  1021.1 18.3 %all-to-all-start = ((bf16[16,48,256]{2,1,0:T(8,128)(2,1)}), bf16[16,48,256]{2,1,0:T(8,128)(2,1)S(1)}, u32[]{:S(2)}, u32[]{:S(2)}) async-start(bf16[16,48,256]{2,1,0:T(8,128)(2,1)} %broadcast_in_dim.123), calls=%async_computation | async-start | bytes 786432 | tf_op jit(solution)/shard_map/while/body/eval_jaxpr/all_to_all | solution.py:12
  1080.4 18.3 %all-to-all-start = ((bf16[16,48,256]{2,1,0:T(8,128)(2,1)}), bf16[16,48,256]{2,1,0:T(8,128)(2,1)S(1)}, u32[]{:S(2)}, u32[]{:S(2)}) async-start(bf16[16,48,256]{2,1,0:T(8,128)(2,1)} %broadcast_in_dim.123), calls=%async_computation | async-start | bytes 786432 | tf_op jit(solution)/shard_map/while/body/eval_jaxpr/all_to_all | solution.py:12
  1139.8 18.3 %all-to-all-start = ((bf16[16,48,256]{2,1,0:T(8,128)(2,1)}), bf16[16,48,256]{2,1,0:T(8,128)(2,1)S(1)}, u32[]{:S(2)}, u32[]{:S(2)}) async-start(bf16[16,48,256]{2,1,0:T(8,128)(2,1)} %broadcast_in_dim.123), calls=%async_computation | async-start | bytes 786432 | tf_op jit(solution)/shard_map/while/body/eval_jaxpr/all_to_all | solution.py:12
  (90 other events, 601.7 us)
Sparse Core Ops, SparseCore 0:
  33.5 39.9 all-gather.3
  77.2 44.8 all-gather.5
where the time goes:
time: 1220 us; the launch traced here: 1200 us
  waiting for transfers between devices  579 us (47%)
  matrix products  177 us (15%)
  starting transfers between devices  171 us (14%)
  local copies, waits for them, and re-layouts  128 us (10%)
  other arithmetic  111 us (9%)
  blocking collectives  23 us (2%)
  between operations  13.5 us (1%)
    all_to_all x18, waiting for transfers between devices, summed_on_arrival(): lax.all_to_all(pieces, axis, split_axis=0, concat_axis=0, tiled=True)  226 us
    all_to_all x18, waiting for transfers between devices, from_everyone(): lax.all_to_all(jnp.broadcast_to(array[None], (peers, *array.shape)), axis...  190 us
    ppermute x18, waiting for transfers between devices, shifted(): lax.ppermute(value, axis, [(source, source + steps) for source in range(f...  89.4 us
    all_to_all x18, starting transfers between devices, from_everyone(): lax.all_to_all(jnp.broadcast_to(array[None], (peers, *array.shape)), axis...  74.2 us
    all_to_all x18, starting transfers between devices, summed_on_arrival(): lax.all_to_all(pieces, axis, split_axis=0, concat_axis=0, tiled=True)  62.1 us
    dot_general x18, matrix products, attention_branch(): key_rows = jnp.dot(normed, w_key, preferred_element_type=jnp.float32)  44.8 us
    dot_general x18, matrix products, attend(): jnp.einsum('hqk,khd->qhd', attn_probs, mixed_values, preferred_element_ty...  40.9 us
    sub x18, matrix products, attend(): expo = jnp.exp(scores - row_top)  40 us
  transfers between devices with their start and end apart: 56, of which 56 were waited for; matrix products, arithmetic and copies ran while one was open for 9% of the time, Pallas kernels for 0%

commit v1 on v0

--- a/solution.py
+++ b/solution.py
@@ -111,7 +111,9 @@
     first_shard = (
         of_everyone(looked.astype(jnp.bfloat16), "section").astype(jnp.float32).astype(jnp.bfloat16)
     )
-    first_full = lax.all_gather(first_shard, "tensor", axis=1, tiled=True)
+    first_full = jnp.concatenate(
+        lax.all_to_all(jnp.stack([first_shard] * lax.axis_size("tensor")), "tensor", 0, 0), axis=1
+    )
     first_float = first_full.astype(jnp.float32)
 
     def root_project():

time: 1220 us -> 1220 us (level)
    all_gather x1 -> x0, waiting for transfers between devices: 37.1 us -> none  [shards(): first_full = lax.all_gather(first_shard, 'tensor', axis=1, tiled=True)]
    all_to_all x0 -> x1, waiting for transfers between devices: none -> 27.7 us  [shards(): lax.all_to_all(jnp.stack([first_shard] * lax.axis_size('tensor')), 'tenso...]
where the time goes in v1:
time: 1220 us; the launch traced here: 1210 us
  waiting for transfers between devices  571 us (47%)
  starting transfers between devices  181 us (15%)
  matrix products  177 us (15%)
  local copies, waits for them, and re-layouts  130 us (11%)
  other arithmetic  108 us (9%)
  blocking collectives  23 us (2%)
  between operations  13.5 us (1%)
    all_to_all x18, waiting for transfers between devices, summed_on_arrival(): lax.all_to_all(pieces, axis, split_axis=0, concat_axis=0, tiled=True)  226 us
    all_to_all x18, waiting for transfers between devices, from_everyone(): lax.all_to_all(jnp.broadcast_to(array[None], (peers, *array.shape)), axis...  190 us
    ppermute x18, waiting for transfers between devices, shifted(): lax.ppermute(value, axis, [(source, source + steps) for source in range(f...  89.4 us
    all_to_all x18, starting transfers between devices, from_everyone(): lax.all_to_all(jnp.broadcast_to(array[None], (peers, *array.shape)), axis...  74.2 us
    all_to_all x18, starting transfers between devices, summed_on_arrival(): lax.all_to_all(pieces, axis, split_axis=0, concat_axis=0, tiled=True)  62.1 us
    dot_general x18, matrix products, attention_branch(): key_rows = jnp.dot(normed, w_key, preferred_element_type=jnp.float32)  44.8 us
    dot_general x18, matrix products, attend(): jnp.einsum('hqk,khd->qhd', attn_probs, mixed_values, preferred_element_ty...  40.9 us
    sub x18, matrix products, attend(): expo = jnp.exp(scores - row_top)  39.6 us
  transfers between devices with their start and end apart: 56, of which 56 were waited for; matrix products, arithmetic and copies ran while one was open for 9% of the time, Pallas kernels for 0%

profile of v1, /device:TPU:3, one launch (start us, length us, event | category | flops | bytes accessed | tf_op | source)
XLA Modules:
  0.0 1206.3 jit_solution(8325237393521581783)
XLA Ops:
  8.2 23.0 %all_to_all.34 = bf16[16,144,256]{2,1,0:T(8,128)(2,1)} all-to-all(bf16[16,144,256]{2,1,0:T(8,128)(2,1)S(1)} %broadcast_in_dim.99), channel_id=1, replica_groups=mesh['section'=16,'tensor'=16] {'section'}, dimensions={0} | all-to-all | bytes 2359296 | tf_op jit(solution)/shard_map/all_to_all | solution.py:12
  48.9 27.7 %all-to-all-done.3 = bf16[16,144,256]{2,1,0:T(8,128)(2,1)} async-done(((bf16[16,144,256]{2,1,0:T(8,128)(2,1)}), bf16[16,144,256]{2,1,0:T(8,128)(2,1)}, u32[]{:S(2)}, u32[]{:S(2)}) %all-to-all-start.3) | async-done | bytes 1179680 | tf_op jit(solution)/shard_map/all_to_all | solution.py:115
  85.6 38.1 %all-gather.3.cloned.1.call-done = bf16[2304,256]{1,0:T(8,128)(2,1)} async-done(((bf16[144,256]{1,0:T(8,128)(2,1)}), bf16[2304,256]{1,0:T(8,128)(2,1)}) %all-gather.3.cloned.1.call-update) | async-done | bytes 1179664 | tf_op jit(solution)/shard_map/all_gather | solution.py:22
  125.8 1073.7 %while.17 = (s32[]{:T(128)}, bf16[48,256]{1,0:T(8,128)(2,1)S(1)}, bf16[3,48,256]{2,1,0:T(8,128)(2,1)}, pred[]{:T(512)}, s32[]{:T(128)}, /*index=5*/bf16[3,48,256...) while((s32[]{:T(128)}, bf16[48,256]{1,0:T(8,128)(2,1)S(1)}, ...), condition=%wide.wide.region_9.10_spmd, body=%wide.wide.region_4.9_spmd.sunk | while | flops 407331392 | bytes 26102732 | solution.py:167
  169.5 12.5 %all-to-all-done.1 = bf16[16,48,256]{2,1,0:T(8,128)(2,1)S(1)} async-done(((bf16[16,48,256]{2,1,0:T(8,128)(2,1)}), bf16[16,48,256]{2,1,0:T(8,128)(2,1)S(1)}, u32[]{:S(2)}, u32[]{:S(2)}) %all-to-all-start.1) | async-done | bytes 393248 | tf_op jit(solution)/shard_map/while/body/eval_jaxpr/all_to_all | solution.py:43
  199.6 10.6 all-to-all-done
  228.8 12.5 %all-to-all-done.1 = bf16[16,48,256]{2,1,0:T(8,128)(2,1)S(1)} async-done(((bf16[16,48,256]{2,1,0:T(8,128)(2,1)}), bf16[16,48,256]{2,1,0:T(8,128)(2,1)S(1)}, u32[]{:S(2)}, u32[]{:S(2)}) %all-to-all-start.1) | async-done | bytes 393248 | tf_op jit(solution)/shard_map/while/body/eval_jaxpr/all_to_all | solution.py:43
  288.2 12.5 %all-to-all-done.1 = bf16[16,48,256]{2,1,0:T(8,128)(2,1)S(1)} async-done(((bf16[16,48,256]{2,1,0:T(8,128)(2,1)}), bf16[16,48,256]{2,1,0:T(8,128)(2,1)S(1)}, u32[]{:S(2)}, u32[]{:S(2)}) %all-to-all-start.1) | async-done | bytes 393248 | tf_op jit(solution)/shard_map/while/body/eval_jaxpr/all_to_all | solution.py:43
  318.3 10.6 all-to-all-done
  347.6 12.5 %all-to-all-done.1 = bf16[16,48,256]{2,1,0:T(8,128)(2,1)S(1)} async-done(((bf16[16,48,256]{2,1,0:T(8,128)(2,1)}), bf16[16,48,256]{2,1,0:T(8,128)(2,1)S(1)}, u32[]{:S(2)}, u32[]{:S(2)}) %all-to-all-start.1) | async-done | bytes 393248 | tf_op jit(solution)/shard_map/while/body/eval_jaxpr/all_to_all | solution.py:43
  406.9 12.5 %all-to-all-done.1 = bf16[16,48,256]{2,1,0:T(8,128)(2,1)S(1)} async-done(((bf16[16,48,256]{2,1,0:T(8,128)(2,1)}), bf16[16,48,256]{2,1,0:T(8,128)(2,1)S(1)}, u32[]{:S(2)}, u32[]{:S(2)}) %all-to-all-start.1) | async-done | bytes 393248 | tf_op jit(solution)/shard_map/while/body/eval_jaxpr/all_to_all | solution.py:43
  466.3 12.5 %all-to-all-done.1 = bf16[16,48,256]{2,1,0:T(8,128)(2,1)S(1)} async-done(((bf16[16,48,256]{2,1,0:T(8,128)(2,1)}), bf16[16,48,256]{2,1,0:T(8,128)(2,1)S(1)}, u32[]{:S(2)}, u32[]{:S(2)}) %all-to-all-start.1) | async-done | bytes 393248 | tf_op jit(solution)/shard_map/while/body/eval_jaxpr/all_to_all | solution.py:43
  525.6 12.5 %all-to-all-done.1 = bf16[16,48,256]{2,1,0:T(8,128)(2,1)S(1)} async-done(((bf16[16,48,256]{2,1,0:T(8,128)(2,1)}), bf16[16,48,256]{2,1,0:T(8,128)(2,1)S(1)}, u32[]{:S(2)}, u32[]{:S(2)}) %all-to-all-start.1) | async-done | bytes 393248 | tf_op jit(solution)/shard_map/while/body/eval_jaxpr/all_to_all | solution.py:43
  585.0 12.5 %all-to-all-done.1 = bf16[16,48,256]{2,1,0:T(8,128)(2,1)S(1)} async-done(((bf16[16,48,256]{2,1,0:T(8,128)(2,1)}), bf16[16,48,256]{2,1,0:T(8,128)(2,1)S(1)}, u32[]{:S(2)}, u32[]{:S(2)}) %all-to-all-start.1) | async-done | bytes 393248 | tf_op jit(solution)/shard_map/while/body/eval_jaxpr/all_to_all | solution.py:43
  644.3 12.5 %all-to-all-done.1 = bf16[16,48,256]{2,1,0:T(8,128)(2,1)S(1)} async-done(((bf16[16,48,256]{2,1,0:T(8,128)(2,1)}), bf16[16,48,256]{2,1,0:T(8,128)(2,1)S(1)}, u32[]{:S(2)}, u32[]{:S(2)}) %all-to-all-start.1) | async-done | bytes 393248 | tf_op jit(solution)/shard_map/while/body/eval_jaxpr/all_to_all | solution.py:43
  703.7 12.5 %all-to-all-done.1 = bf16[16,48,256]{2,1,0:T(8,128)(2,1)S(1)} async-done(((bf16[16,48,256]{2,1,0:T(8,128)(2,1)}), bf16[16,48,256]{2,1,0:T(8,128)(2,1)S(1)}, u32[]{:S(2)}, u32[]{:S(2)}) %all-to-all-start.1) | async-done | bytes 393248 | tf_op jit(solution)/shard_map/while/body/eval_jaxpr/all_to_all | solution.py:43
  763.1 12.5 %all-to-all-done.1 = bf16[16,48,256]{2,1,0:T(8,128)(2,1)S(1)} async-done(((bf16[16,48,256]{2,1,0:T(8,128)(2,1)}), bf16[16,48,256]{2,1,0:T(8,128)(2,1)S(1)}, u32[]{:S(2)}, u32[]{:S(2)}) %all-to-all-start.1) | async-done | bytes 393248 | tf_op jit(solution)/shard_map/while/body/eval_jaxpr/all_to_all | solution.py:43
  822.4 12.5 %all-to-all-done.1 = bf16[16,48,256]{2,1,0:T(8,128)(2,1)S(1)} async-done(((bf16[16,48,256]{2,1,0:T(8,128)(2,1)}), bf16[16,48,256]{2,1,0:T(8,128)(2,1)S(1)}, u32[]{:S(2)}, u32[]{:S(2)}) %all-to-all-start.1) | async-done | bytes 393248 | tf_op jit(solution)/shard_map/while/body/eval_jaxpr/all_to_all | solution.py:43
  881.8 12.5 %all-to-all-done.1 = bf16[16,48,256]{2,1,0:T(8,128)(2,1)S(1)} async-done(((bf16[16,48,256]{2,1,0:T(8,128)(2,1)}), bf16[16,48,256]{2,1,0:T(8,128)(2,1)S(1)}, u32[]{:S(2)}, u32[]{:S(2)}) %all-to-all-start.1) | async-done | bytes 393248 | tf_op jit(solution)/shard_map/while/body/eval_jaxpr/all_to_all | solution.py:43
  941.2 12.5 %all-to-all-done.1 = bf16[16,48,256]{2,1,0:T(8,128)(2,1)S(1)} async-done(((bf16[16,48,256]{2,1,0:T(8,128)(2,1)}), bf16[16,48,256]{2,1,0:T(8,128)(2,1)S(1)}, u32[]{:S(2)}, u32[]{:S(2)}) %all-to-all-start.1) | async-done | bytes 393248 | tf_op jit(solution)/shard_map/while/body/eval_jaxpr/all_to_all | solution.py:43
  1000.5 12.5 %all-to-all-done.1 = bf16[16,48,256]{2,1,0:T(8,128)(2,1)S(1)} async-done(((bf16[16,48,256]{2,1,0:T(8,128)(2,1)}), bf16[16,48,256]{2,1,0:T(8,128)(2,1)S(1)}, u32[]{:S(2)}, u32[]{:S(2)}) %all-to-all-start.1) | async-done | bytes 393248 | tf_op jit(solution)/shard_map/while/body/eval_jaxpr/all_to_all | solution.py:43
  1059.9 12.5 %all-to-all-done.1 = bf16[16,48,256]{2,1,0:T(8,128)(2,1)S(1)} async-done(((bf16[16,48,256]{2,1,0:T(8,128)(2,1)}), bf16[16,48,256]{2,1,0:T(8,128)(2,1)S(1)}, u32[]{:S(2)}, u32[]{:S(2)}) %all-to-all-start.1) | async-done | bytes 393248 | tf_op jit(solution)/shard_map/while/body/eval_jaxpr/all_to_all | solution.py:43
  1119.2 12.5 %all-to-all-done.1 = bf16[16,48,256]{2,1,0:T(8,128)(2,1)S(1)} async-done(((bf16[16,48,256]{2,1,0:T(8,128)(2,1)}), bf16[16,48,256]{2,1,0:T(8,128)(2,1)S(1)}, u32[]{:S(2)}, u32[]{:S(2)}) %all-to-all-start.1) | async-done | bytes 393248 | tf_op jit(solution)/shard_map/while/body/eval_jaxpr/all_to_all | solution.py:43
  1178.6 12.5 %all-to-all-done.1 = bf16[16,48,256]{2,1,0:T(8,128)(2,1)S(1)} async-done(((bf16[16,48,256]{2,1,0:T(8,128)(2,1)}), bf16[16,48,256]{2,1,0:T(8,128)(2,1)S(1)}, u32[]{:S(2)}, u32[]{:S(2)}) %all-to-all-start.1) | async-done | bytes 393248 | tf_op jit(solution)/shard_map/while/body/eval_jaxpr/all_to_all | solution.py:43
  (620 shorter events, 854.8 us)
Async XLA Ops:
  35.3 41.3 %all-to-all-start.3 = ((bf16[16,144,256]{2,1,0:T(8,128)(2,1)}), bf16[16,144,256]{2,1,0:T(8,128)(2,1)}, u32[]{:S(2)}, u32[]{:S(2)}) async-start(bf16[16,144,256]{2,1,0:T(8,128)(2,1)} %stack.2), calls=%async_computation.3 | async-start | bytes 2359296 | tf_op jit(solution)/shard_map/all_to_all | solution.py:115
  45.9 77.7 %all-gather.3.cloned.1.call-start = ((), (), s32[]{:S(2)}) async-start(), calls=%async_computation.4 | async-start | bytes 1253376 | tf_op jit(solution)/shard_map/all_gather | solution.py:22
  127.3 23.5 %all-to-all-start = ((bf16[16,48,256]{2,1,0:T(8,128)(2,1)}), bf16[16,48,256]{2,1,0:T(8,128)(2,1)S(1)}, u32[]{:S(2)}, u32[]{:S(2)}) async-start(bf16[16,48,256]{2,1,0:T(8,128)(2,1)} %broadcast_in_dim.123), calls=%async_computation | async-start | bytes 786432 | tf_op jit(solution)/shard_map/while/body/eval_jaxpr/all_to_all | solution.py:12
  164.7 17.4 %all-to-all-start.1 = ((bf16[16,48,256]{2,1,0:T(8,128)(2,1)}), bf16[16,48,256]{2,1,0:T(8,128)(2,1)S(1)}, u32[]{:S(2)}, u32[]{:S(2)}) async-start(bf16[16,48,256]{2,1,0:T(8,128)(2,1)} %bitcast.135), calls=%async_computation.1 | async-start | bytes 786432 | tf_op jit(solution)/shard_map/while/body/eval_jaxpr/all_to_all | solution.py:43
  191.9 18.3 %all-to-all-start = ((bf16[16,48,256]{2,1,0:T(8,128)(2,1)}), bf16[16,48,256]{2,1,0:T(8,128)(2,1)S(1)}, u32[]{:S(2)}, u32[]{:S(2)}) async-start(bf16[16,48,256]{2,1,0:T(8,128)(2,1)} %broadcast_in_dim.123), calls=%async_computation | async-start | bytes 786432 | tf_op jit(solution)/shard_map/while/body/eval_jaxpr/all_to_all | solution.py:12
  251.2 18.3 %all-to-all-start = ((bf16[16,48,256]{2,1,0:T(8,128)(2,1)}), bf16[16,48,256]{2,1,0:T(8,128)(2,1)S(1)}, u32[]{:S(2)}, u32[]{:S(2)}) async-start(bf16[16,48,256]{2,1,0:T(8,128)(2,1)} %broadcast_in_dim.123), calls=%async_computation | async-start | bytes 786432 | tf_op jit(solution)/shard_map/while/body/eval_jaxpr/all_to_all | solution.py:12
  283.4 17.4 %all-to-all-start.1 = ((bf16[16,48,256]{2,1,0:T(8,128)(2,1)}), bf16[16,48,256]{2,1,0:T(8,128)(2,1)S(1)}, u32[]{:S(2)}, u32[]{:S(2)}) async-start(bf16[16,48,256]{2,1,0:T(8,128)(2,1)} %bitcast.135), calls=%async_computation.1 | async-start | bytes 786432 | tf_op jit(solution)/shard_map/while/body/eval_jaxpr/all_to_all | solution.py:43
  310.6 18.3 %all-to-all-start = ((bf16[16,48,256]{2,1,0:T(8,128)(2,1)}), bf16[16,48,256]{2,1,0:T(8,128)(2,1)S(1)}, u32[]{:S(2)}, u32[]{:S(2)}) async-start(bf16[16,48,256]{2,1,0:T(8,128)(2,1)} %broadcast_in_dim.123), calls=%async_computation | async-start | bytes 786432 | tf_op jit(solution)/shard_map/while/body/eval_jaxpr/all_to_all | solution.py:12
  369.9 18.3 %all-to-all-start = ((bf16[16,48,256]{2,1,0:T(8,128)(2,1)}), bf16[16,48,256]{2,1,0:T(8,128)(2,1)S(1)}, u32[]{:S(2)}, u32[]{:S(2)}) async-start(bf16[16,48,256]{2,1,0:T(8,128)(2,1)} %broadcast_in_dim.123), calls=%async_computation | async-start | bytes 786432 | tf_op jit(solution)/shard_map/while/body/eval_jaxpr/all_to_all | solution.py:12
  402.1 17.4 %all-to-all-start.1 = ((bf16[16,48,256]{2,1,0:T(8,128)(2,1)}), bf16[16,48,256]{2,1,0:T(8,128)(2,1)S(1)}, u32[]{:S(2)}, u32[]{:S(2)}) async-start(bf16[16,48,256]{2,1,0:T(8,128)(2,1)} %bitcast.135), calls=%async_computation.1 | async-start | bytes 786432 | tf_op jit(solution)/shard_map/while/body/eval_jaxpr/all_to_all | solution.py:43
  429.3 18.3 %all-to-all-start = ((bf16[16,48,256]{2,1,0:T(8,128)(2,1)}), bf16[16,48,256]{2,1,0:T(8,128)(2,1)S(1)}, u32[]{:S(2)}, u32[]{:S(2)}) async-start(bf16[16,48,256]{2,1,0:T(8,128)(2,1)} %broadcast_in_dim.123), calls=%async_computation | async-start | bytes 786432 | tf_op jit(solution)/shard_map/while/body/eval_jaxpr/all_to_all | solution.py:12
  488.7 18.3 %all-to-all-start = ((bf16[16,48,256]{2,1,0:T(8,128)(2,1)}), bf16[16,48,256]{2,1,0:T(8,128)(2,1)S(1)}, u32[]{:S(2)}, u32[]{:S(2)}) async-start(bf16[16,48,256]{2,1,0:T(8,128)(2,1)} %broadcast_in_dim.123), calls=%async_computation | async-start | bytes 786432 | tf_op jit(solution)/shard_map/while/body/eval_jaxpr/all_to_all | solution.py:12
  520.8 17.4 %all-to-all-start.1 = ((bf16[16,48,256]{2,1,0:T(8,128)(2,1)}), bf16[16,48,256]{2,1,0:T(8,128)(2,1)S(1)}, u32[]{:S(2)}, u32[]{:S(2)}) async-start(bf16[16,48,256]{2,1,0:T(8,128)(2,1)} %bitcast.135), calls=%async_computation.1 | async-start | bytes 786432 | tf_op jit(solution)/shard_map/while/body/eval_jaxpr/all_to_all | solution.py:43
  548.0 18.3 %all-to-all-start = ((bf16[16,48,256]{2,1,0:T(8,128)(2,1)}), bf16[16,48,256]{2,1,0:T(8,128)(2,1)S(1)}, u32[]{:S(2)}, u32[]{:S(2)}) async-start(bf16[16,48,256]{2,1,0:T(8,128)(2,1)} %broadcast_in_dim.123), calls=%async_computation | async-start | bytes 786432 | tf_op jit(solution)/shard_map/while/body/eval_jaxpr/all_to_all | solution.py:12
  607.4 18.3 %all-to-all-start = ((bf16[16,48,256]{2,1,0:T(8,128)(2,1)}), bf16[16,48,256]{2,1,0:T(8,128)(2,1)S(1)}, u32[]{:S(2)}, u32[]{:S(2)}) async-start(bf16[16,48,256]{2,1,0:T(8,128)(2,1)} %broadcast_in_dim.123), calls=%async_computation | async-start | bytes 786432 | tf_op jit(solution)/shard_map/while/body/eval_jaxpr/all_to_all | solution.py:12
  666.8 18.3 %all-to-all-start = ((bf16[16,48,256]{2,1,0:T(8,128)(2,1)}), bf16[16,48,256]{2,1,0:T(8,128)(2,1)S(1)}, u32[]{:S(2)}, u32[]{:S(2)}) async-start(bf16[16,48,256]{2,1,0:T(8,128)(2,1)} %broadcast_in_dim.123), calls=%async_computation | async-start | bytes 786432 | tf_op jit(solution)/shard_map/while/body/eval_jaxpr/all_to_all | solution.py:12
  726.1 18.3 %all-to-all-start = ((bf16[16,48,256]{2,1,0:T(8,128)(2,1)}), bf16[16,48,256]{2,1,0:T(8,128)(2,1)S(1)}, u32[]{:S(2)}, u32[]{:S(2)}) async-start(bf16[16,48,256]{2,1,0:T(8,128)(2,1)} %broadcast_in_dim.123), calls=%async_computation | async-start | bytes 786432 | tf_op jit(solution)/shard_map/while/body/eval_jaxpr/all_to_all | solution.py:12
  785.5 18.3 %all-to-all-start = ((bf16[16,48,256]{2,1,0:T(8,128)(2,1)}), bf16[16,48,256]{2,1,0:T(8,128)(2,1)S(1)}, u32[]{:S(2)}, u32[]{:S(2)}) async-start(bf16[16,48,256]{2,1,0:T(8,128)(2,1)} %broadcast_in_dim.123), calls=%async_computation | async-start | bytes 786432 | tf_op jit(solution)/shard_map/while/body/eval_jaxpr/all_to_all | solution.py:12
  844.8 18.3 %all-to-all-start = ((bf16[16,48,256]{2,1,0:T(8,128)(2,1)}), bf16[16,48,256]{2,1,0:T(8,128)(2,1)S(1)}, u32[]{:S(2)}, u32[]{:S(2)}) async-start(bf16[16,48,256]{2,1,0:T(8,128)(2,1)} %broadcast_in_dim.123), calls=%async_computation | async-start | bytes 786432 | tf_op jit(solution)/shard_map/while/body/eval_jaxpr/all_to_all | solution.py:12
  904.2 18.3 %all-to-all-start = ((bf16[16,48,256]{2,1,0:T(8,128)(2,1)}), bf16[16,48,256]{2,1,0:T(8,128)(2,1)S(1)}, u32[]{:S(2)}, u32[]{:S(2)}) async-start(bf16[16,48,256]{2,1,0:T(8,128)(2,1)} %broadcast_in_dim.123), calls=%async_computation | async-start | bytes 786432 | tf_op jit(solution)/shard_map/while/body/eval_jaxpr/all_to_all | solution.py:12
  963.5 18.3 %all-to-all-start = ((bf16[16,48,256]{2,1,0:T(8,128)(2,1)}), bf16[16,48,256]{2,1,0:T(8,128)(2,1)S(1)}, u32[]{:S(2)}, u32[]{:S(2)}) async-start(bf16[16,48,256]{2,1,0:T(8,128)(2,1)} %broadcast_in_dim.123), calls=%async_computation | async-start | bytes 786432 | tf_op jit(solution)/shard_map/while/body/eval_jaxpr/all_to_all | solution.py:12
  1022.9 18.3 %all-to-all-start = ((bf16[16,48,256]{2,1,0:T(8,128)(2,1)}), bf16[16,48,256]{2,1,0:T(8,128)(2,1)S(1)}, u32[]{:S(2)}, u32[]{:S(2)}) async-start(bf16[16,48,256]{2,1,0:T(8,128)(2,1)} %broadcast_in_dim.123), calls=%async_computation | async-start | bytes 786432 | tf_op jit(solution)/shard_map/while/body/eval_jaxpr/all_to_all | solution.py:12
  1082.3 18.3 %all-to-all-start = ((bf16[16,48,256]{2,1,0:T(8,128)(2,1)}), bf16[16,48,256]{2,1,0:T(8,128)(2,1)S(1)}, u32[]{:S(2)}, u32[]{:S(2)}) async-start(bf16[16,48,256]{2,1,0:T(8,128)(2,1)} %broadcast_in_dim.123), calls=%async_computation | async-start | bytes 786432 | tf_op jit(solution)/shard_map/while/body/eval_jaxpr/all_to_all | solution.py:12
  1141.6 18.3 %all-to-all-start = ((bf16[16,48,256]{2,1,0:T(8,128)(2,1)}), bf16[16,48,256]{2,1,0:T(8,128)(2,1)S(1)}, u32[]{:S(2)}, u32[]{:S(2)}) async-start(bf16[16,48,256]{2,1,0:T(8,128)(2,1)} %broadcast_in_dim.123), calls=%async_computation | async-start | bytes 786432 | tf_op jit(solution)/shard_map/while/body/eval_jaxpr/all_to_all | solution.py:12
  (90 other events, 576.7 us)
Sparse Core Ops, SparseCore 0:
  77.4 46.1 all-gather.2
